TPU v7x, 128 devices: a whole 4x4x4 slice. The times are simulated.
128 devices in a mesh: ep: 8 (over x, core), fsdp: 16 (over z, y).
Axes of the slice: x: 4, y: 4, z: 4, core: 2. Of those that a mesh axis runs over, the one named last changes fastest.
Arguments:
- master_gate: float32 [128, 2048, 768], P('ep', 'fsdp'), may hold values from -0.1875 to 0.1875
- master_up: float32 [128, 2048, 768], P('ep', 'fsdp'), may hold values from -0.1875 to 0.1875
- router_weight: float32 [2048, 128], P('fsdp', 'ep'), may hold values from -0.125 to 0.125
- router_gain: float32 [2048], P('fsdp'), may hold values from 0.25 to 1.75
Outputs:
- final_gate: bfloat16 [128, 2048, 768], P(('ep', 'fsdp'))
- final_up: bfloat16 [128, 2048, 768], P(('ep', 'fsdp'))
- scale_gate: float32 [128, 768], P(('ep', 'fsdp'))
- scale_up: float32 [128, 768], P(('ep', 'fsdp'))
- serve_router: bfloat16 [2048, 128], replicated
All inputs are finite; a program needn't handle non-finite values.
Results may differ from a plain program's by a relative error of at most 0.001.
Values may be sent and summed in bfloat16 or wider, within the bound.
A program may use at most 128 MiB of HBM per device.

v0:
```python
import jax
import jax.numpy as jnp
from jax import lax
from jax.sharding import Mesh
from jax.sharding import PartitionSpec as P

EP = ("ep_0", "ep_1")
EP_FSDP = ("ep_0", "ep_1", "fsdp")


def copy_for_each(value, axis):
    devices = lax.axis_size(axis)
    return lax.all_to_all(
        jnp.broadcast_to(value[None], (devices, *value.shape)), axis, 0, 0, tiled=True
    )


def taken_together(value, axis):
    return copy_for_each(value, axis).sum(axis=0)


def in_one(arrays, axis):
    ends = [0]
    for a in arrays:
        ends.append(ends[-1] + a.size)
    so_far = taken_together(jnp.concatenate([a.ravel() for a in arrays]), axis)
    return tuple((so_far[b:e].reshape(a.shape) for a, b, e in zip(arrays, ends, ends[1:])))


def sent_together(arrays, axis, split_dim, concat_dim, along):
    ends, at = ([], 0)
    for a in arrays[:-1]:
        at += a.shape[along]
        ends.append(at)
    both = jnp.concatenate(arrays, axis=along)
    return tuple(
        jnp.split(
            lax.all_to_all(both, axis, split_axis=split_dim, concat_axis=concat_dim, tiled=True),
            ends,
            axis=along,
        )
    )


def joined_along(parts, dim):
    dims = list(parts.shape[1:])
    dims[dim] *= parts.shape[0]
    return jnp.moveaxis(parts, 0, dim).reshape(dims)


def gather_directly(value, axis, dim):
    return joined_along(copy_for_each(value, axis), dim)


def gather_in_order(value, axes, sequence):
    parts = value[None]
    for k in sequence:
        parts = lax.all_gather(parts, axes[k], axis=0, tiled=True)
    block = [lax.axis_size(axes[k]) for k in reversed(sequence)]
    parts = parts.reshape(*block, *value.shape)
    turned = sorted(range(len(sequence)), key=lambda place: sequence[len(sequence) - 1 - place])
    return parts.transpose(*turned, *range(len(sequence), parts.ndim)).reshape(-1, *value.shape)


def gather_axes(value, axes, sequence, dim):
    return joined_along(gather_in_order(value, axes, sequence), dim)


def body(master_gate, master_up, router_weight, router_gain):
    total_gate, total_up = in_one(
        (jnp.sum(master_gate * master_gate, axis=1), jnp.sum(master_up * master_up, axis=1)), "fsdp"
    )
    scale_gate = jnp.sqrt(total_gate)
    scale_up = jnp.sqrt(total_up)
    narrow_gate, narrow_up = (
        (master_gate / jnp.expand_dims(scale_gate, 1)).astype(jnp.bfloat16),
        (master_up / jnp.expand_dims(scale_up, 1)).astype(jnp.bfloat16),
    )
    final_gate, final_up = sent_together((narrow_gate, narrow_up), "fsdp", 0, 1, 2)
    scale_gate = lax.dynamic_slice_in_dim(
        scale_gate, lax.axis_index("fsdp") * final_gate.shape[0], final_gate.shape[0], axis=0
    )
    scale_up = lax.dynamic_slice_in_dim(
        scale_up, lax.axis_index("fsdp") * final_up.shape[0], final_up.shape[0], axis=0
    )
    part_router = (router_weight * router_gain[:, None]).astype(jnp.bfloat16)
    row_router = gather_directly(part_router, "fsdp", 0)
    serve_router = gather_axes(row_router, ("ep_0", "ep_1"), (0, 1), 1)
    return (final_gate, final_up, scale_gate, scale_up, serve_router)


def solution(mesh):
    finer = Mesh(mesh.devices.reshape(4, 2, mesh.shape["fsdp"]), ("ep_0", "ep_1", "fsdp"))
    return jax.shard_map(
        body,
        mesh=finer,
        in_specs=(P(EP, "fsdp", None), P(EP, "fsdp", None), P("fsdp", EP), P("fsdp")),
        out_specs=(
            P(EP_FSDP, None, None),
            P(EP_FSDP, None, None),
            P(EP_FSDP, None),
            P(EP_FSDP, None),
            P(),
        ),
        check_vma=False,
    )
```

profile of v0, /device:TPU:0, one launch (start us, length us, event | category | flops | bytes accessed | tf_op | source)
XLA Modules:
  0.0 161.2 jit_solution(398515752994868322)
XLA Ops:
  0.6 3.3 %multiply_reduce_fusion.1 = f32[16,768]{1,0:T(8,128)S(1)} fusion(f32[16,128,768]{2,1,0:T(8,128)} %param.4), kind=kLoop, calls=%fused_computation.4 | loop fusion | flops 3133440 | bytes 6340608 | tf_op jit(solution)/shard_map/reduce_sum | solution.py:71
  4.0 0.0 copy-start
  4.0 0.0 copy-start.1
  4.0 3.3 %multiply_reduce_fusion = f32[16,768]{1,0:T(8,128)S(1)} fusion(f32[16,128,768]{2,1,0:T(8,128)} %param.5), kind=kLoop, calls=%fused_computation.3 | loop fusion | flops 3133440 | bytes 6340608 | tf_op jit(solution)/shard_map/reduce_sum | solution.py:71
  7.4 2.4 %broadcast_in_dim.4 = f32[16,1,24576]{2,1,0:T(1,128)} broadcast(f32[24576]{0:T(1024)S(1)} %pad_maximum_fusion.1), dimensions={2} | broadcast | bytes 1671168 | tf_op jit(solution)/shard_map/broadcast_in_dim | solution.py:14
  9.7 8.2 %all-to-all-start = ((f32[16,1,24576]{2,1,0:T(1,128)}), f32[16,1,24576]{2,1,0:T(1,128)S(1)}, u32[]{:S(2)}, u32[]{:S(2)}) async-start(f32[16,1,24576]{2,1,0:T(1,128)} %broadcast_in_dim.4), calls=%async_computation | async-start | bytes 3145728 | tf_op jit(solution)/shard_map/all_to_all | solution.py:13
  17.9 0.0 copy-done
  17.9 0.0 copy-done.1
  17.9 24.5 %all-to-all-done = f32[16,1,24576]{2,1,0:T(1,128)S(1)} async-done(((f32[16,1,24576]{2,1,0:T(1,128)}), f32[16,1,24576]{2,1,0:T(1,128)S(1)}, u32[]{:S(2)}, u32[]{:S(2)}) %all-to-all-start) | async-done | bytes 1572896 | tf_op jit(solution)/shard_map/all_to_all | solution.py:13
  42.4 0.6 broadcast_in_dim.5
  43.1 3.5 %all-to-all-start.2 = ((bf16[16,128,16]{1,2,0:T(8,128)(2,1)}), bf16[16,128,16]{1,2,0:T(8,128)(2,1)S(1)}, u32[]{:S(2)}, u32[]{:S(2)}) async-start(bf16[16,128,16]{1,2,0:T(8,128)(2,1)} %broadcast_in_dim.5), calls=%async_computation.2 | async-start | bytes 131072 | tf_op jit(solution)/shard_map/all_to_all | solution.py:13
  46.6 1.0 reduce_sum.29
  47.7 5.3 %divide_convert_fusion = (bf16[16,128,768]{2,1,0:T(8,128)(2,1)S(1)}, bf16[16,128,768]{2,1,0:T(8,128)(2,1)S(1)}) fusion(f32[16,128,768]{2,1,0:T(8,128)} %param.5, f32[16,768]{1,0:T(8,128)S(1)} %sqrt.15, f32[16,128,768]{2,1,0:T(8,128)} %param.4, f32[16,768]{1,0:T(8,128)S(1)} %sqrt.13), kind=kLoop, calls=%fused_computation.1 | loop fusion | flops 6291456 | bytes 18972672 | tf_op jit(solution)/shard_map/convert_element_type | solution.py:77
  53.0 3.2 %pad_maximum_fusion = bf16[16,128,1536]{2,1,0:T(8,128)(2,1)} fusion(bf16[16,128,768]{2,1,0:T(8,128)(2,1)S(1)} %get-tuple-element.39, bf16[16,128,768]{2,1,0:T(8,128)(2,1)S(1)} %get-tuple-element.40), kind=kLoop, calls=%fused_computation | loop fusion | flops 12582912 | bytes 12582912 | tf_op jit(solution)/shard_map/concatenate | solution.py:35
  56.2 0.0 all-to-all-done.2
  56.2 7.2 %all-to-all-start.1 = ((bf16[16,128,1536]{2,1,0:T(8,128)(2,1)}), bf16[16,128,1536]{2,1,0:T(8,128)(2,1)}, u32[]{:S(2)}, u32[]{:S(2)}) async-start(bf16[16,128,1536]{2,1,0:T(8,128)(2,1)} %pad_maximum_fusion), calls=%async_computation.1 | async-start | bytes 12582912 | tf_op jit(solution)/shard_map/all_to_all | solution.py:38
  63.5 12.7 %all_gather.6 = bf16[4,2048,16]{1,2,0:T(8,128)(2,1)S(1)} all-gather(bf16[1,2048,16]{1,2,0:T(8,128)(2,1)S(1)} %broadcast_in_dim_reshape.3), channel_id=1, replica_groups=mesh['ep_0'=4,'ep_1'=2,'fsdp'=16] {'ep_0'}, dimensions={0}, use_global_device_ids=true | all-gather | bytes 327680 | tf_op jit(solution)/shard_map/all_gather | solution.py:58
  76.2 2.2 %all_gather.7 = bf16[8,2048,16]{1,2,0:T(8,128)(2,1)S(1)} all-gather(bf16[4,2048,16]{1,2,0:T(8,128)(2,1)S(1)} %all_gather.6), channel_id=1, replica_groups=mesh['ep_0'=4,'ep_1'=2,'fsdp'=16] {'ep_1'}, dimensions={0}, use_global_device_ids=true | all-gather | bytes 786432 | tf_op jit(solution)/shard_map/all_gather | solution.py:58
  78.4 1.0 copy.24
  79.4 0.6 constant_dynamic-slice_fusion
  80.0 75.3 %all-to-all-done.1 = bf16[16,128,1536]{2,1,0:T(8,128)(2,1)} async-done(((bf16[16,128,1536]{2,1,0:T(8,128)(2,1)}), bf16[16,128,1536]{2,1,0:T(8,128)(2,1)}, u32[]{:S(2)}, u32[]{:S(2)}) %all-to-all-start.1) | async-done | bytes 6291488 | tf_op jit(solution)/shard_map/all_to_all | solution.py:38
  155.2 5.9 %fusion = (bf16[1,2048,768]{2,1,0:T(8,128)(2,1)}, bf16[1,2048,768]{2,1,0:T(8,128)(2,1)}) fusion(bf16[1,2048,1536]{2,1,0:T(8,128)(2,1)} %bitcast), kind=kLoop, calls=%fused_computation.11 | loop fusion | bytes 12582912 | tf_op jit(solution)/shard_map/split | solution.py:37
  (10 shorter events, 0.2 us)
Async XLA Ops:
  4.0 13.9 %copy-start = (f32[128,16]{0,1:T(8,128)S(1)}, f32[128,16]{0,1:T(8,128)}, u32[]{:S(2)}) copy-start(f32[128,16]{0,1:T(8,128)} %param.6) | copy-start | bytes 24580
  4.0 13.9 %copy-start.1 = (f32[128]{0:T(128)S(1)}, f32[128]{0:T(128)}, u32[]{:S(2)}) copy-start(f32[128]{0:T(128)} %param.7) | copy-start | bytes 1540
  9.7 32.7 %all-to-all-start = ((f32[16,1,24576]{2,1,0:T(1,128)}), f32[16,1,24576]{2,1,0:T(1,128)S(1)}, u32[]{:S(2)}, u32[]{:S(2)}) async-start(f32[16,1,24576]{2,1,0:T(1,128)} %broadcast_in_dim.4), calls=%async_computation | async-start | bytes 3145728 | tf_op jit(solution)/shard_map/all_to_all | solution.py:13
  43.1 13.2 %all-to-all-start.2 = ((bf16[16,128,16]{1,2,0:T(8,128)(2,1)}), bf16[16,128,16]{1,2,0:T(8,128)(2,1)S(1)}, u32[]{:S(2)}, u32[]{:S(2)}) async-start(bf16[16,128,16]{1,2,0:T(8,128)(2,1)} %broadcast_in_dim.5), calls=%async_computation.2 | async-start | bytes 131072 | tf_op jit(solution)/shard_map/all_to_all | solution.py:13
  56.2 99.0 %all-to-all-start.1 = ((bf16[16,128,1536]{2,1,0:T(8,128)(2,1)}), bf16[16,128,1536]{2,1,0:T(8,128)(2,1)}, u32[]{:S(2)}, u32[]{:S(2)}) async-start(bf16[16,128,1536]{2,1,0:T(8,128)(2,1)} %pad_maximum_fusion), calls=%async_computation.1 | async-start | bytes 12582912 | tf_op jit(solution)/shard_map/all_to_all | solution.py:38
where the time goes:
time: 162 us; the launch traced here: 161 us
  waiting for transfers between devices  99.7 us (62%)
  starting transfers between devices  18.9 us (12%)
  other arithmetic  16.2 us (10%)
  blocking collectives  14.8 us (9%)
  local copies, waits for them, and re-layouts  10.7 us (7%)
    all_to_all x1, waiting for transfers between devices, sent_together(): lax.all_to_all(both, axis, split_axis=split_dim, concat_axis=concat_dim,...  75.3 us
    all_to_all x2, waiting for transfers between devices, copy_for_each(): lax.all_to_all(jnp.broadcast_to(value[None], (devices, *value.shape)), ax...  24.5 us
    all_gather x2, blocking collectives, gather_in_order(): parts = lax.all_gather(parts, axes[k], axis=0, tiled=True)  14.8 us
    all_to_all x2, starting transfers between devices, copy_for_each(): lax.all_to_all(jnp.broadcast_to(value[None], (devices, *value.shape)), ax...  11.7 us
    all_to_all x1, starting transfers between devices, sent_together(): lax.all_to_all(both, axis, split_axis=split_dim, concat_axis=concat_dim,...  7.2 us
    split x1, local copies, waits for them, and re-layouts, sent_together(): jnp.split(lax.all_to_all(both, axis, split_axis=split_dim, concat_axis=co...  5.95 us
    convert_element_type x1, other arithmetic, body(): (master_up / jnp.expand_dims(scale_up, 1)).astype(jnp.bfloat16)  5.31 us
    reduce_sum x1, other arithmetic, body(): jnp.sum(master_gate * master_gate, axis=1)  3.33 us
  transfers between devices with their start and end apart: 3, of which 2 were waited for; matrix products, arithmetic and copies ran while one was open for 7% of the time, Pallas kernels for 0%

commit v1 on v0

--- a/solution.py
+++ b/solution.py
@@ -55,7 +55,9 @@
 def gather_in_order(value, axes, sequence):
     parts = value[None]
     for k in sequence:
-        parts = lax.all_gather(parts, axes[k], axis=0, tiled=True)
+        parts = jnp.concatenate(
+            lax.all_to_all(jnp.stack([parts] * lax.axis_size(axes[k])), axes[k], 0, 0), axis=0
+        )
     block = [lax.axis_size(axes[k]) for k in reversed(sequence)]
     parts = parts.reshape(*block, *value.shape)
     turned = sorted(range(len(sequence)), key=lambda place: sequence[len(sequence) - 1 - place])

time: 162 us -> 180 us (1.11)
  waiting for transfers between devices: 99.7 us -> 125 us
  blocking collectives: 14.8 us -> 0 us
  starting transfers between devices: 18.9 us -> 25.3 us
  local copies, waits for them, and re-layouts: 10.7 us -> 12.5 us
    all_to_all x1, waiting for transfers between devices: 75.3 us -> 95.3 us  [sent_together(): lax.all_to_all(both, axis, split_axis=split_dim, concat_axis=concat_dim,...]
    all_gather x2 -> x0, blocking collectives: 14.8 us -> none  [gather_in_order(): parts = lax.all_gather(parts, axes[k], axis=0, tiled=True)]
    all_to_all x0 -> x2, starting transfers between devices: none -> 7.78 us  [gather_in_order(): lax.all_to_all(jnp.stack([parts] * lax.axis_size(axes[k])), axes[k], 0, 0)]
    all_to_all x0 -> x2, waiting for transfers between devices: none -> 6.67 us  [gather_in_order(): lax.all_to_all(jnp.stack([parts] * lax.axis_size(axes[k])), axes[k], 0, 0)]
    reduce_sum x1, other arithmetic: 3.33 us -> 0.54 us  [body(): jnp.sum(master_up * master_up, axis=1)]
    all_to_all x1, starting transfers between devices: 7.2 us -> 4.65 us  [sent_together(): lax.all_to_all(both, axis, split_axis=split_dim, concat_axis=concat_dim,...]
  transfers between devices with their start and end apart: 3 -> 5, of which waited for: 2 -> 4; matrix products, arithmetic and copies ran while one was open for 7% -> 9% of each run, Pallas kernels for 0% -> 0%
where the time goes in v1:
time: 180 us; the launch traced here: 179 us
  waiting for transfers between devices  125 us (69%)
  starting transfers between devices  25.3 us (14%)
  other arithmetic  15.1 us (8%)
  local copies, waits for them, and re-layouts  12.5 us (7%)
    all_to_all x1, waiting for transfers between devices, sent_together(): lax.all_to_all(both, axis, split_axis=split_dim, concat_axis=concat_dim,...  95.3 us
    all_to_all x2, waiting for transfers between devices, copy_for_each(): lax.all_to_all(jnp.broadcast_to(value[None], (devices, *value.shape)), ax...  23.4 us
    all_to_all x2, starting transfers between devices, copy_for_each(): lax.all_to_all(jnp.broadcast_to(value[None], (devices, *value.shape)), ax...  12.9 us
    all_to_all x2, starting transfers between devices, gather_in_order(): lax.all_to_all(jnp.stack([parts] * lax.axis_size(axes[k])), axes[k], 0, 0)  7.78 us
    all_to_all x2, waiting for transfers between devices, gather_in_order(): lax.all_to_all(jnp.stack([parts] * lax.axis_size(axes[k])), axes[k], 0, 0)  6.67 us
    split x1, local copies, waits for them, and re-layouts, sent_together(): jnp.split(lax.all_to_all(both, axis, split_axis=split_dim, concat_axis=co...  5.95 us
    convert_element_type x1, other arithmetic, body(): (master_up / jnp.expand_dims(scale_up, 1)).astype(jnp.bfloat16)  5.31 us
    all_to_all x1, starting transfers between devices, sent_together(): lax.all_to_all(both, axis, split_axis=split_dim, concat_axis=concat_dim,...  4.65 us
  transfers between devices with their start and end apart: 5, of which 4 were waited for; matrix products, arithmetic and copies ran while one was open for 9% of the time, Pallas kernels for 0%

profile of v1, /device:TPU:0, one launch (start us, length us, event | category | flops | bytes accessed | tf_op | source)
XLA Modules:
  0.0 179.0 jit_solution(4801421026315068205)
XLA Ops:
  0.6 0.7 multiply_convert_fusion
  1.3 0.6 broadcast_in_dim.5
  2.0 8.2 %all-to-all-start.2 = ((bf16[16,128,16]{1,2,0:T(8,128)(2,1)}), bf16[16,128,16]{1,2,0:T(8,128)(2,1)S(1)}, u32[]{:S(2)}, u32[]{:S(2)}) async-start(bf16[16,128,16]{1,2,0:T(8,128)(2,1)} %broadcast_in_dim.5), calls=%async_computation.2 | async-start | bytes 131072 | tf_op jit(solution)/shard_map/all_to_all | solution.py:13
  10.1 0.0 copy-start
  10.2 3.5 %multiply_reduce_fusion.1 = f32[16,768]{1,0:T(8,128)S(1)} fusion(f32[16,128,768]{2,1,0:T(8,128)} %param.4), kind=kLoop, calls=%fused_computation.4 | loop fusion | flops 3133440 | bytes 6340608 | tf_op jit(solution)/shard_map/reduce_sum | solution.py:73
  13.6 1.1 copy-done
  14.7 0.5 multiply_reduce_fusion
  15.3 2.5 %all-to-all-done.2 = bf16[16,128,16]{1,2,0:T(8,128)(2,1)S(1)} async-done(((bf16[16,128,16]{1,2,0:T(8,128)(2,1)}), bf16[16,128,16]{1,2,0:T(8,128)(2,1)S(1)}, u32[]{:S(2)}, u32[]{:S(2)}) %all-to-all-start.2) | async-done | bytes 65568 | tf_op jit(solution)/shard_map/all_to_all | solution.py:13
  17.8 0.7 stack.6
  18.5 4.3 %all-to-all-start.3 = ((bf16[4,1,2048,16]{2,3,1,0:T(8,128)(2,1)}), bf16[4,1,2048,16]{2,3,1,0:T(8,128)(2,1)S(1)}, u32[]{:S(2)}, u32[]{:S(2)}) async-start(bf16[4,1,2048,16]{2,3,1,0:T(8,128)(2,1)} %stack.6), calls=%async_computation.3 | async-start | bytes 524288 | tf_op jit(solution)/shard_map/all_to_all | solution.py:59
  22.8 6.7 %all-to-all-done.3 = bf16[4,1,2048,16]{2,3,1,0:T(8,128)(2,1)S(1)} async-done(((bf16[4,1,2048,16]{2,3,1,0:T(8,128)(2,1)}), bf16[4,1,2048,16]{2,3,1,0:T(8,128)(2,1)S(1)}, u32[]{:S(2)}, u32[]{:S(2)}) %all-to-all-start.3) | async-done | bytes 262176 | tf_op jit(solution)/shard_map/all_to_all | solution.py:59
  29.5 2.4 %broadcast_in_dim.4 = f32[16,1,24576]{2,1,0:T(1,128)} broadcast(f32[24576]{0:T(1024)S(1)} %pad_maximum_fusion.2), dimensions={2} | broadcast | bytes 1671168 | tf_op jit(solution)/shard_map/broadcast_in_dim | solution.py:14
  31.9 4.7 %all-to-all-start = ((f32[16,1,24576]{2,1,0:T(1,128)}), f32[16,1,24576]{2,1,0:T(1,128)S(1)}, u32[]{:S(2)}, u32[]{:S(2)}) async-start(f32[16,1,24576]{2,1,0:T(1,128)} %broadcast_in_dim.4), calls=%async_computation | async-start | bytes 3145728 | tf_op jit(solution)/shard_map/all_to_all | solution.py:13
  36.6 0.8 pad_maximum_fusion.1
  37.4 20.9 %all-to-all-done = f32[16,1,24576]{2,1,0:T(1,128)S(1)} async-done(((f32[16,1,24576]{2,1,0:T(1,128)}), f32[16,1,24576]{2,1,0:T(1,128)S(1)}, u32[]{:S(2)}, u32[]{:S(2)}) %all-to-all-start) | async-done | bytes 1572896 | tf_op jit(solution)/shard_map/all_to_all | solution.py:13
  58.3 3.5 %all-to-all-start.4 = ((bf16[2,4,2048,16]{2,3,1,0:T(8,128)(2,1)}), bf16[2,4,2048,16]{2,3,1,0:T(8,128)(2,1)S(1)}, u32[]{:S(2)}, u32[]{:S(2)}) async-start(bf16[2,4,2048,16]{2,3,1,0:T(8,128)(2,1)} %pad_maximum_fusion.1), calls=%async_computation.4 | async-start | bytes 1048576 | tf_op jit(solution)/shard_map/all_to_all | solution.py:59
  61.8 1.0 reduce_sum.29
  62.9 5.3 %divide_convert_fusion = (bf16[16,128,768]{2,1,0:T(8,128)(2,1)S(1)}, bf16[16,128,768]{2,1,0:T(8,128)(2,1)S(1)}) fusion(f32[16,128,768]{2,1,0:T(8,128)} %param.5, f32[16,768]{1,0:T(8,128)S(1)} %sqrt.15, f32[16,128,768]{2,1,0:T(8,128)} %param.4, f32[16,768]{1,0:T(8,128)S(1)} %sqrt.13), kind=kLoop, calls=%fused_computation.1 | loop fusion | flops 6291456 | bytes 18972672 | tf_op jit(solution)/shard_map/convert_element_type | solution.py:79
  68.3 3.2 %pad_maximum_fusion = bf16[16,128,1536]{2,1,0:T(8,128)(2,1)} fusion(bf16[16,128,768]{2,1,0:T(8,128)(2,1)S(1)} %get-tuple-element.39, bf16[16,128,768]{2,1,0:T(8,128)(2,1)S(1)} %get-tuple-element.40), kind=kLoop, calls=%fused_computation | loop fusion | flops 12582912 | bytes 12582912 | tf_op jit(solution)/shard_map/concatenate | solution.py:35
  71.5 0.0 all-to-all-done.4
  71.5 4.6 %all-to-all-start.1 = ((bf16[16,128,1536]{2,1,0:T(8,128)(2,1)}), bf16[16,128,1536]{2,1,0:T(8,128)(2,1)}, u32[]{:S(2)}, u32[]{:S(2)}) async-start(bf16[16,128,1536]{2,1,0:T(8,128)(2,1)} %pad_maximum_fusion), calls=%async_computation.1 | async-start | bytes 12582912 | tf_op jit(solution)/shard_map/all_to_all | solution.py:38
  76.2 1.0 copy.24
  77.2 0.6 constant_dynamic-slice_fusion
  77.8 95.3 %all-to-all-done.1 = bf16[16,128,1536]{2,1,0:T(8,128)(2,1)} async-done(((bf16[16,128,1536]{2,1,0:T(8,128)(2,1)}), bf16[16,128,1536]{2,1,0:T(8,128)(2,1)}, u32[]{:S(2)}, u32[]{:S(2)}) %all-to-all-start.1) | async-done | bytes 6291488 | tf_op jit(solution)/shard_map/all_to_all | solution.py:38
  173.1 5.9 %fusion = (bf16[1,2048,768]{2,1,0:T(8,128)(2,1)}, bf16[1,2048,768]{2,1,0:T(8,128)(2,1)}) fusion(bf16[1,2048,1536]{2,1,0:T(8,128)(2,1)} %bitcast), kind=kLoop, calls=%fused_computation.13 | loop fusion | bytes 12582912 | tf_op jit(solution)/shard_map/split | solution.py:37
  (8 shorter events, 0.1 us)
Async XLA Ops:
  2.0 15.8 %all-to-all-start.2 = ((bf16[16,128,16]{1,2,0:T(8,128)(2,1)}), bf16[16,128,16]{1,2,0:T(8,128)(2,1)S(1)}, u32[]{:S(2)}, u32[]{:S(2)}) async-start(bf16[16,128,16]{1,2,0:T(8,128)(2,1)} %broadcast_in_dim.5), calls=%async_computation.2 | async-start | bytes 131072 | tf_op jit(solution)/shard_map/all_to_all | solution.py:13
  10.1 4.6 %copy-start = (f32[16,128,768]{2,1,0:T(8,128)S(1)}, f32[16,128,768]{2,1,0:T(8,128)}, u32[]{:S(2)}) copy-start(f32[16,128,768]{2,1,0:T(8,128)} %param.5) | copy-start | bytes 18874372
  18.5 11.0 %all-to-all-start.3 = ((bf16[4,1,2048,16]{2,3,1,0:T(8,128)(2,1)}), bf16[4,1,2048,16]{2,3,1,0:T(8,128)(2,1)S(1)}, u32[]{:S(2)}, u32[]{:S(2)}) async-start(bf16[4,1,2048,16]{2,3,1,0:T(8,128)(2,1)} %stack.6), calls=%async_computation.3 | async-start | bytes 524288 | tf_op jit(solution)/shard_map/all_to_all | solution.py:59
  31.9 26.5 %all-to-all-start = ((f32[16,1,24576]{2,1,0:T(1,128)}), f32[16,1,24576]{2,1,0:T(1,128)S(1)}, u32[]{:S(2)}, u32[]{:S(2)}) async-start(f32[16,1,24576]{2,1,0:T(1,128)} %broadcast_in_dim.4), calls=%async_computation | async-start | bytes 3145728 | tf_op jit(solution)/shard_map/all_to_all | solution.py:13
  58.3 13.1 %all-to-all-start.4 = ((bf16[2,4,2048,16]{2,3,1,0:T(8,128)(2,1)}), bf16[2,4,2048,16]{2,3,1,0:T(8,128)(2,1)S(1)}, u32[]{:S(2)}, u32[]{:S(2)}) async-start(bf16[2,4,2048,16]{2,3,1,0:T(8,128)(2,1)} %pad_maximum_fusion.1), calls=%async_computation.4 | async-start | bytes 1048576 | tf_op jit(solution)/shard_map/all_to_all | solution.py:59
  71.5 101.6 %all-to-all-start.1 = ((bf16[16,128,1536]{2,1,0:T(8,128)(2,1)}), bf16[16,128,1536]{2,1,0:T(8,128)(2,1)}, u32[]{:S(2)}, u32[]{:S(2)}) async-start(bf16[16,128,1536]{2,1,0:T(8,128)(2,1)} %pad_maximum_fusion), calls=%async_computation.1 | async-start | bytes 12582912 | tf_op jit(solution)/shard_map/all_to_all | solution.py:38
